TPU v7x, 32 devices: a whole 2x2x4 slice. The times are simulated.
32 devices in a mesh: section: 16 (over z, x, core), tp: 2 (over y).
Axes of the slice: x: 2, y: 2, z: 4, core: 2. Of those that a mesh axis runs over, the one named last changes fastest.
Arguments:
- carried: bfloat16 [16, 256, 5120], P('section', 'tp'), may hold values from -6 to 6
- carried_segments: int32 [16, 256], P('section'), may hold values from 0 to 31, as said below
- fresh_batch: bfloat16 [2, 256, 5120], P(None, 'tp'), may hold values from -6 to 6
- fresh_segments: int32 [2, 256], replicated, may hold values from 0 to 31, as said below
- qkv_weight: bfloat16 [16, 5120, 3, 2048], P('section', None, None, 'tp'), may hold values from -3.354102 to 3.354102
- out_weight: bfloat16 [16, 2048, 5120], P('section', 'tp'), may hold values from -0.09375 to 0.09375
- norm_gain: bfloat16 [16, 2560], P('section'), may hold values from 0.099609375 to 1.8984375
Outputs:
- layer_outputs: bfloat16 [2, 16, 256, 5120], P(None, 'section', 'tp')
- shadow_outputs: bfloat16 [16, 256, 5120], P('section', 'tp')
Inputs may be any that keep to these rules, and one draw needn't show every extreme that they name: `carried_segments`: document ids of each micro-batch's 512 tokens, read in token order across its two halves, start at 0, never fall, and rise by one at each document start; every micro-batch holds exactly 32 documents. `fresh_segments`: the same law for the entering micro-batch.
All inputs are finite; a program needn't handle non-finite values.
Results may differ from a plain program's by a relative error of at most 0.019.
Values may be sent and summed in bfloat16 or wider, within the bound.
A program may use at most 128 MiB of HBM per device.

v0:
```python
import functools

import jax
import jax.numpy as jnp
import numpy as np
from jax import lax
from jax.experimental import pallas as pl
from jax.experimental.pallas import tpu as pltpu
from jax.sharding import PartitionSpec as P

HD = 128
LANES = 128
LOG2E = 1.4426950408889634
TILE = 512
CHUNK = 1024
PARTS = 2
NORM_ROWS = 16
SEND_AT = 5
RELAY_AT = 3
MESH = pl.DeviceIdType.MESH

eps = 1e-05
rope_base = 10000.0


def relay_kernel(
    groups,
    sections,
    x_hbm,
    segments_hbm,
    fresh_hbm,
    fresh_segments_hbm,
    weights_in_hbm,
    weights_out_hbm,
    gain_hbm,
    cosine_hbm,
    sine_hbm,
    out_hbm,
    shadow_hbm,
    weights_in,
    weights_out,
    gathered,
    qkv,
    mixed,
    kept,
    give_out,
    give_in,
    arrived,
    rows_in,
    staged,
    cosine,
    sine,
    bias,
    pieces,
    ids,
    gain_raw,
    gain_pieces,
    gain,
    load_sem,
    tile_sem,
    chunk_sem,
    own_row_sem,
    next_row_sem,
    small_send,
    small_recv,
    own_send,
    own_recv,
    share_send,
    share_recv,
    relay_send,
    relay_recv,
    give_send,
    give_recv,
    sum_send,
    sum_recv,
    shift_send,
    shift_recv,
    back_send,
    back_recv,
    store_sem,
    free_sem,
):
    place = lax.axis_index("section")
    mine = lax.axis_index("tp")
    parity = place % 2
    core = (place + 1 - 2 * parity, mine)
    has_next, has_previous = place + 2 < sections, place >= 2
    ahead, behind = (place + 2, mine), (place - 2, mine)

    block, depth = x_hbm.shape
    half = block * groups
    tiles, _, tile = weights_in.shape
    per_kind = tiles // 3
    chunks, width, chunk = weights_out.shape
    heads = width // HD
    part = block // PARTS

    def peer(by):
        return (mine + by) % groups

    def source(by):
        return (mine + groups - by) % groups

    def block_at(index):
        return pl.ds(pl.multiple_of(index * block, block), block)

    def remote(src, dst, send, recv, device):
        return pltpu.make_async_remote_copy(
            src_ref=src, dst_ref=dst, send_sem=send, recv_sem=recv, device_id=device, device_id_type=MESH
        )

    def tile_copy(j):
        kind = j // per_kind
        columns = pl.ds(pl.multiple_of((j % per_kind) * tile, tile), tile)
        return pltpu.make_async_copy(weights_in_hbm.at[kind, :, columns], weights_in.at[j], tile_sem.at[j])

    def columns_of(c):
        return pl.ds(pl.multiple_of(c * chunk, chunk), chunk)

    def chunk_copy(c):
        return pltpu.make_async_copy(weights_out_hbm.at[:, columns_of(c)], weights_out.at[c], chunk_sem.at[c])

    def own_rows_copy(c):
        return pltpu.make_async_copy(x_hbm.at[:, columns_of(c)], rows_in.at[0, c], own_row_sem.at[c])

    def fresh_copy(c):
        return pltpu.make_async_copy(
            fresh_hbm.at[parity, :, columns_of(c)], rows_in.at[1, c], next_row_sem.at[c]
        )

    gain_copy = pltpu.make_async_copy(gain_hbm, gain_raw, load_sem.at[0])
    ids_copy = pltpu.make_async_copy(segments_hbm, pieces.at[parity], load_sem.at[1])
    cosine_copy = pltpu.make_async_copy(cosine_hbm, cosine, load_sem.at[2])
    sine_copy = pltpu.make_async_copy(sine_hbm, sine, load_sem.at[3])
    fresh_ids_copy = pltpu.make_async_copy(fresh_segments_hbm, ids.at[1], load_sem.at[4])

    gain_send = remote(gain_pieces.at[parity], gain_pieces.at[parity], small_send.at[0], small_recv.at[0], core)
    ids_send = remote(pieces.at[parity], pieces.at[parity], small_send.at[1], small_recv.at[1], core)
    ids_ahead = remote(ids.at[0], ids.at[1], small_send.at[2], small_recv.at[2], ahead)

    gain_copy.start()
    ids_copy.start()
    for c in range(chunks):
        own_rows_copy(c).start()
    for j in range(tiles):
        tile_copy(j).start()
    cosine_copy.start()
    sine_copy.start()
    for c in range(chunks):
        chunk_copy(c).start()

    @pl.when(jnp.logical_not(has_previous))
    def _():
        fresh_ids_copy.start()
        for c in range(chunks):
            fresh_copy(c).start()

    barrier = pltpu.get_barrier_semaphore()
    pl.semaphore_signal(barrier, inc=1, device_id=core, device_id_type=MESH)
    for g in range(1, groups):
        pl.semaphore_signal(barrier, inc=1, device_id=(place, peer(g)), device_id_type=MESH)

    @pl.when(has_next)
    def _():
        pl.semaphore_signal(barrier, inc=1, device_id=ahead, device_id_type=MESH)

    @pl.when(has_previous)
    def _():
        pl.semaphore_signal(barrier, inc=1, device_id=behind, device_id_type=MESH)

    pl.semaphore_wait(barrier, groups + has_next.astype(jnp.int32) + has_previous.astype(jnp.int32))

    gain_copy.wait()
    gain_pieces[parity] = gain_raw[...].astype(jnp.float32)
    gain_send.start()
    ids_copy.wait()
    ids_send.start()

    def normalize(step):
        def some(r, carry):
            rows = pl.ds(pl.multiple_of(r * NORM_ROWS, NORM_ROWS), NORM_ROWS)
            power = jnp.zeros((NORM_ROWS, 1), jnp.float32)
            for c in range(chunks):
                widened = rows_in[step, c, rows, :].astype(jnp.float32)
                power = power + jnp.sum(widened * widened, axis=-1, keepdims=True)
            scale = lax.rsqrt(power / depth + eps)
            target = pl.ds(pl.multiple_of(parity * block + r * NORM_ROWS, NORM_ROWS), NORM_ROWS)
            for c in range(chunks):
                columns = slice(c * chunk, (c + 1) * chunk)
                widened = rows_in[step, c, rows, :].astype(jnp.float32)
                gathered[mine, target, columns] = (widened * scale * gain[:, columns]).astype(jnp.bfloat16)
            return carry

        lax.fori_loop(0, block // NORM_ROWS, some, 0)

    def own_copy():
        rows = gathered.at[mine, pl.ds(pl.multiple_of(parity * block, block), block)]
        return remote(rows, rows, own_send.at[0], own_recv.at[0], core)

    def share_copy(g, s):
        rows = gathered.at[mine, pl.ds(pl.multiple_of(parity * block + s * part, part), part)]
        slot = (g - 1) * PARTS + s
        return remote(rows, rows, share_send.at[slot], share_recv.at[slot], (place, peer(g)))

    def relay_copy(g, s, h):
        rows = gathered.at[source(g), pl.ds(h * block + s * part, part)]
        slot = (g - 1) * PARTS + s
        return remote(rows, rows, relay_send.at[slot], relay_recv.at[slot], core)

    def share():
        for s in range(PARTS):
            for g in range(1, groups):
                share_copy(g, s).start()

    def relay(s, h):
        for g in range(1, groups):
            share_copy(g, s).wait_recv()
            relay_copy(g, s, h).start()

    def project(rows, places, first, events):
        def one(j, carry):
            for at, event in events:
                pl.when(j == at)(event)
            if first:
                tile_copy(j).wait()
            kind = j // per_kind
            turning = (kind < 2).astype(jnp.float32)
            factor = turning * jnp.where(kind == 0, HD ** (-0.5) * LOG2E, 1.0)
            product = jnp.dot(rows(), weights_in[j], preferred_element_type=jnp.float32)
            column = (j % per_kind) * tile
            for i, token in enumerate(places):
                at = pl.ds(pl.multiple_of(token, block), block)
                cosines = cosine[at, :] * factor + (1.0 - turning)
                sines = sine[at, :] * factor
                for n in range(tile // HD):
                    each = product[i * block : (i + 1) * block, n * HD : (n + 1) * HD]
                    turned = each * cosines + pltpu.roll(each, HD // 2, 1) * sines
                    to = pl.ds(pl.multiple_of(column + n * HD, HD), HD)
                    qkv[kind, at, to] = turned.astype(jnp.bfloat16)
            return carry

        lax.fori_loop(0, tiles, one, 0)

    def project_others(h):
        def one(g, carry):
            index = source(g)
            project(
                lambda: gathered[index, h * block : (h + 1) * block, :],
                [h * half + index * block],
                False,
                [],
            )
            return carry

        lax.fori_loop(1, groups, one, 0)

    def find_bias(step):
        across = half // LANES
        for h in range(2):
            row = jnp.broadcast_to(ids[step, h : h + 1, :].astype(jnp.float32), (LANES, half))
            column = row.T
            for q in range(across):
                wanted = column[q * LANES : (q + 1) * LANES]
                first = h * half + q * LANES
                for k in range(h * across + q + 1):
                    given = ids[step, k // across : k // across + 1, (k % across) * LANES : (k % across + 1) * LANES]
                    seen = wanted == given.astype(jnp.float32)
                    if k == h * across + q:
                        down = lax.broadcasted_iota(jnp.int32, (LANES, LANES), 0)
                        seen = seen & (lax.broadcasted_iota(jnp.int32, (LANES, LANES), 1) <= down)
                    bias[first : first + LANES, k * LANES : (k + 1) * LANES] = jnp.where(seen, 0.0, -1e30)

    def attend(h):
        def one(n, carry):
            to = pl.ds(pl.multiple_of(n * HD, HD), HD)
            for q in range(half // LANES):
                first = h * half + q * LANES
                last = first + LANES
                scores = lax.dot_general(
                    qkv[0, first:last, to],
                    qkv[1, 0:last, to],
                    (((1,), (1,)), ((), ())),
                    preferred_element_type=jnp.float32,
                ) + bias[first:last, 0:last]
                weights = jnp.exp2(scores - jnp.max(scores, axis=-1, keepdims=True))
                total = jnp.sum(weights, axis=-1, keepdims=True)
                product = jnp.dot(
                    weights.astype(jnp.bfloat16), qkv[2, 0:last, to], preferred_element_type=jnp.float32
                )
                mixed[q * LANES : (q + 1) * LANES, to] = (product / total).astype(jnp.bfloat16)
            return carry

        lax.fori_loop(0, heads, one, 0, unroll=2)

    def give_copy(i):
        g, c = (i // chunks + 1) % groups, i % chunks
        slot = i % 2
        return remote(
            give_out.at[slot], give_in.at[c, block_at(peer(g))], give_send.at[slot], give_recv.at[i], core
        )

    def out_product(i):
        g, c = (i // chunks + 1) % groups, i % chunks
        return jnp.dot(mixed[block_at(peer(g)), :], weights_out[c], preferred_element_type=jnp.float32)

    messages = groups * chunks

    def give():
        def one(i, carry):
            @pl.when(i >= 2)
            def _():
                give_copy(i).wait_send()

            give_out[i % 2] = out_product(i).astype(jnp.bfloat16)
            give_copy(i).start()
            return carry

        lax.fori_loop(0, messages, one, 0)
        give_copy(messages - 2).wait_send()
        give_copy(messages - 1).wait_send()

    def sum_copy(i):
        g, c = i // chunks + 1, i % chunks
        return remote(
            give_in.at[c, block_at(peer(g))], arrived.at[c, g - 1], sum_send.at[i], sum_recv.at[i], (place, peer(g))
        )

    def keep_others():
        def one(i, carry):
            g, c = i // chunks + 1, i % chunks
            give_copy(i).wait_recv()
            total = out_product(i) + give_in[c, block_at(peer(g)), :].astype(jnp.float32)
            give_in[c, block_at(peer(g)), :] = total.astype(jnp.bfloat16)
            sum_copy(i).start()
            return carry

        lax.fori_loop(0, messages - chunks, one, 0)

    def keep_own(step):
        def one(i, carry):
            c = i % chunks
            give_copy(i).wait_recv()
            total = out_product(i) + give_in[c, block_at(mine), :].astype(jnp.float32)
            kept[c] = total + rows_in[step, c].astype(jnp.float32)
            return carry

        lax.fori_loop(messages - chunks, messages, one, 0)

    def store_copy(step, c):
        return pltpu.make_async_copy(staged.at[c], out_hbm.at[step, 0, :, columns_of(c)], store_sem.at[c])

    def shift_copy(c):
        return remote(staged.at[c], rows_in.at[1, c], shift_send.at[c], shift_recv.at[c], ahead)

    def back_copy(c):
        return remote(
            staged.at[c], shadow_hbm.at[0, :, columns_of(c)], back_send.at[c], back_recv.at[c], behind
        )

    def finish(step, low, high):
        def one(c, carry):
            total = kept[c]
            for g in range(1, groups):
                sum_copy((g - 1) * chunks + c).wait_recv()
                total = total + arrived[c, g - 1].astype(jnp.float32)
            staged[c] = total.astype(jnp.bfloat16)
            if step == 0:
                pl.when(has_next)(lambda: shift_copy(c).start())
            else:
                pl.when(has_previous)(lambda: back_copy(c).start())
            store_copy(step, c).start()
            return carry

        lax.fori_loop(low, high, one, 0)

    def zero_copy(c):
        return pltpu.make_async_copy(staged.at[0], shadow_hbm.at[0, :, columns_of(c)], back_recv.at[c])

    def wait_sent(copies):
        for copy in copies:
            copy.wait_send()

    every_share = [(g, s) for g in range(1, groups) for s in range(PARTS)]
    is_low, is_high = parity == 0, parity == 1

    ids_send.wait_recv()
    ids[0, 0:1, :] = pieces[0]
    ids[0, 1:2, :] = pieces[1]
    pl.when(has_next)(ids_ahead.start)
    gain_send.wait_recv()
    gain[:, 0 : depth // 2] = gain_pieces[0]
    gain[:, depth // 2 :] = gain_pieces[1]
    for c in range(chunks):
        own_rows_copy(c).wait()
    normalize(0)
    own_copy().start()
    pl.when(is_low)(share)

    @pl.when(jnp.logical_not(has_next))
    def _():
        staged[0] = jnp.zeros_like(staged[0])
        for c in range(chunks):
            zero_copy(c).start()

    cosine_copy.wait()
    sine_copy.wait()
    find_bias(0)

    for step in range(2):
        own_copy().wait_recv()

        def send_high():
            pl.when(is_high)(share)

        def relay_low():
            pl.when(is_low)(lambda: relay(0, 0))

        project(
            lambda: gathered[mine],
            [mine * block, half + mine * block],
            step == 0,
            [(min(RELAY_AT, tiles - 1), relay_low), (min(SEND_AT, tiles - 1), send_high)],
        )

        if step == 0:

            @pl.when(jnp.logical_not(has_next))
            def _():
                for c in range(chunks):
                    zero_copy(c).wait()

            for c in range(chunks):
                chunk_copy(c).wait()

        @pl.when(is_low)
        def _():
            for s in range(1, PARTS):
                relay(s, 0)

        @pl.when(is_high)
        def _():
            for g, s in every_share:
                relay_copy(g, s, 0).wait_recv()

        project_others(0)
        attend(0)

        @pl.when(is_low)
        def _():
            wait_sent([relay_copy(g, s, 0) for g, s in every_share])
            keep_others()
            keep_own(step)

        @pl.when(is_high)
        def _():
            give()
            for s in range(PARTS):
                relay(s, 1)

        @pl.when(is_low)
        def _():
            for g, s in every_share:
                relay_copy(g, s, 1).wait_recv()

        project_others(1)

        @pl.when(is_low)
        def _():
            finish(step, 0, 2)

        attend(1)

        @pl.when(is_low)
        def _():
            give()
            finish(step, 2, chunks)

        @pl.when(is_high)
        def _():
            wait_sent([relay_copy(g, s, 1) for g, s in every_share])
            keep_others()
            keep_own(step)
            finish(step, 0, chunks)

        wait_sent([sum_copy(i) for i in range(messages - chunks)])
        if step == 0:

            @pl.when(is_high)
            def _():
                pl.semaphore_signal(free_sem, inc=1, device_id=core, device_id_type=MESH)

        own_copy().wait_send()
        wait_sent([share_copy(g, s) for g, s in every_share])
        for c in range(chunks):
            store_copy(step, c).wait()
        if step == 0:

            @pl.when(has_next)
            def _():
                ids_ahead.wait_send()
                wait_sent([shift_copy(c) for c in range(chunks)])

            @pl.when(has_previous)
            def _():
                ids_ahead.wait_recv()
                for c in range(chunks):
                    shift_copy(c).wait_recv()

            @pl.when(jnp.logical_not(has_previous))
            def _():
                fresh_ids_copy.wait()
                for c in range(chunks):
                    fresh_copy(c).wait()

            normalize(1)
            own_copy().start()

            @pl.when(is_low)
            def _():
                pl.semaphore_wait(free_sem, 1)
                share()

            find_bias(1)

    gain_send.wait_send()
    ids_send.wait_send()

    @pl.when(has_previous)
    def _():
        wait_sent([back_copy(c) for c in range(chunks)])

    @pl.when(has_next)
    def _():
        for c in range(chunks):
            back_copy(c).wait_recv()


def turning(tokens):
    dim = HD // 2
    frequency = np.float32(rope_base) ** (-(np.arange(dim, dtype=np.float32) * np.float32(2.0 / HD)))
    angles = np.arange(tokens, dtype=np.float32)[:, None] * frequency.astype(np.float32)[None, :]
    cosine, sine = np.cos(angles), np.sin(angles)
    return (
        np.concatenate([cosine, cosine], -1).astype(np.float32),
        np.concatenate([-sine, sine], -1).astype(np.float32),
    )


def per_device(
    groups, sections, carried, carried_segments, fresh_batch, fresh_segments, qkv_weight, out_weight, norm_gain
):
    block, depth = carried.shape[1:]
    half = block * groups
    width = out_weight.shape[1]
    tile = min(TILE, width)
    tiles = 3 * width // tile
    chunks = depth // CHUNK
    cosine, sine = turning(2 * half)
    weights_in = jnp.transpose(qkv_weight[0], (1, 0, 2))
    near, f32 = jnp.bfloat16, jnp.float32
    dma = pltpu.SemaphoreType.DMA
    shares = (groups - 1) * PARTS
    messages = groups * chunks
    flops = 2 * (2 * 2 * half * depth * 4 * width + 4 * width * 4 * half * half)
    out, shadow = pl.pallas_call(
        functools.partial(relay_kernel, groups, sections),
        out_shape=(
            jax.ShapeDtypeStruct((2, 1, block, depth), near),
            jax.ShapeDtypeStruct((1, block, depth), near),
        ),
        in_specs=[pl.BlockSpec(memory_space=pl.ANY)] * 9,
        out_specs=(pl.BlockSpec(memory_space=pl.ANY),) * 2,
        scratch_shapes=[
            pltpu.VMEM((tiles, depth, tile), near),
            pltpu.VMEM((chunks, width, CHUNK), near),
            pltpu.VMEM((groups, 2 * block, depth), near),
            pltpu.VMEM((3, 2 * half, width), near),
            pltpu.VMEM((half, width), near),
            pltpu.VMEM((chunks, block, CHUNK), f32),
            pltpu.VMEM((2, block, CHUNK), near),
            pltpu.VMEM((chunks, half, CHUNK), near),
            pltpu.VMEM((chunks, groups - 1, block, CHUNK), near),
            pltpu.VMEM((2, chunks, block, CHUNK), near),
            pltpu.VMEM((chunks, block, CHUNK), near),
            pltpu.VMEM((2 * half, HD), f32),
            pltpu.VMEM((2 * half, HD), f32),
            pltpu.VMEM((2 * half, 2 * half), f32),
            pltpu.VMEM((2, 1, half), jnp.int32),
            pltpu.VMEM((2, 2, half), jnp.int32),
            pltpu.VMEM((1, depth // 2), near),
            pltpu.VMEM((2, 1, depth // 2), f32),
            pltpu.VMEM((1, depth), f32),
            dma((5,)),
            dma((tiles,)),
            dma((chunks,)),
            dma((chunks,)),
            dma((chunks,)),
            dma((3,)),
            dma((3,)),
            dma((1,)),
            dma((1,)),
            dma((shares,)),
            dma((shares,)),
            dma((shares,)),
            dma((shares,)),
            dma((2,)),
            dma((messages,)),
            dma((messages - chunks,)),
            dma((messages - chunks,)),
            dma((chunks,)),
            dma((chunks,)),
            dma((chunks,)),
            dma((chunks,)),
            dma((chunks,)),
            pltpu.SemaphoreType.REGULAR,
        ],
        compiler_params=pltpu.CompilerParams(
            collective_id=0, has_side_effects=True, vmem_limit_bytes=67043328
        ),
        cost_estimate=pl.CostEstimate(
            flops=flops, bytes_accessed=8 * depth * width, transcendentals=0
        ),
        name="relay",
    )(
        carried[0],
        carried_segments,
        fresh_batch,
        fresh_segments,
        weights_in,
        out_weight[0],
        norm_gain,
        cosine,
        sine,
    )
    return out, shadow


def solution(mesh):
    return jax.shard_map(
        functools.partial(per_device, mesh.shape["tp"], mesh.shape["section"]),
        mesh=mesh,
        in_specs=(
            P("section", "tp", None),
            P("section", None),
            P(None, "tp", None),
            P(),
            P("section", None, None, "tp"),
            P("section", "tp", None),
            P("section", None),
        ),
        out_specs=(P(None, "section", "tp", None), P("section", "tp", None)),
        check_vma=False,
    )
```

profile of v0, /device:TPU:1, one launch (start us, length us, event | category | flops | bytes accessed | tf_op | source)
XLA Modules:
  0.0 180.3 jit_solution(17538203556883704422)
XLA Ops:
  0.6 175.1 %relay.1 = (bf16[2,1,128,5120]{3,2,1,0:T(8,128)(2,1)}, bf16[1,128,5120]{2,1,0:T(8,128)(2,1)}) custom-call(bf16[128,5120]{1,0:T(8,128)(2,1)} %bitcast.7, s32[1,256]{1,0:T(1,128)} %segments_hbm.1, bf16[2,128,5120]{2,1,0:T(8,128)(2,1)} %fresh_hbm.1, s32[2,256]{1,0:T(2,128)} %fresh_segments_hbm.1, bf16[3,5120,1024]{2,1,0:T(8,128)(2,1)} %bitcast.5, ...), custom_call_target="tpu_custom_call" | custom-call | flops 45097156608 | bytes 41943040 | tf_op jit(solution)/shard_map/relay/pallas_call | solution.py:565
  175.8 0.0 copy-start
  175.8 3.5 %copy.13 = bf16[2,1,128,5120]{3,2,1,0:T(8,128)(2,1)} copy(bf16[2,1,128,5120]{3,2,1,0:T(8,128)(2,1)} %get-tuple-element.4) | data formatting | bytes 5242880
  179.3 0.0 copy-done
  179.3 1.1 copy.14
Async XLA Ops:
  175.8 3.5 %copy-start = (bf16[1,128,5120]{2,1,0:T(8,128)(2,1)S(1)}, bf16[1,128,5120]{2,1,0:T(8,128)(2,1)}, u32[]{:S(2)}) copy-start(bf16[1,128,5120]{2,1,0:T(8,128)(2,1)} %get-tuple-element.5) | copy-start | bytes 3932164
where the time goes:
time: 180 us
  Pallas kernels  175 us (97%)
  local copies, waits for them, and re-layouts  4.56 us (3%)
    pallas_call x1, Pallas kernels, per_device(): pl.pallas_call(functools.partial(relay_kernel, groups, sections), out_sha...  175 us
    unnamed x4, local copies, waits for them, and re-layouts  4.56 us

commit v1 on v0

--- a/solution.py
+++ b/solution.py
@@ -13,10 +13,14 @@
 LOG2E = 1.4426950408889634
 TILE = 512
 CHUNK = 1024
-PARTS = 2
+PARTS = 4
 NORM_ROWS = 16
-SEND_AT = 5
-RELAY_AT = 3
+PIECE = 256
+RELAYS_AT = ((3, 5), (0, 0, 3))
+COMBINES_AT = (1, 2, 3)
+FREE_AT = 3
+SHARE_AT = 4
+FINISH_AT = 4
 MESH = pl.DeviceIdType.MESH
 
 eps = 1e-05
@@ -42,8 +46,7 @@
     gathered,
     qkv,
     mixed,
-    kept,
-    give_out,
+    partial,
     give_in,
     arrived,
     rows_in,
@@ -142,10 +145,32 @@
     ids_copy.start()
     for c in range(chunks):
         own_rows_copy(c).start()
+    cosine_copy.start()
+    sine_copy.start()
+
+    barrier = pltpu.get_barrier_semaphore()
+    pl.semaphore_signal(barrier, inc=1, device_id=core, device_id_type=MESH)
+    for g in range(1, groups):
+        pl.semaphore_signal(barrier, inc=1, device_id=(place, peer(g)), device_id_type=MESH)
+
+    @pl.when(has_next)
+    def _():
+        pl.semaphore_signal(barrier, inc=1, device_id=ahead, device_id_type=MESH)
+
+    @pl.when(has_previous)
+    def _():
+        pl.semaphore_signal(barrier, inc=1, device_id=behind, device_id_type=MESH)
+
+    with jax.named_scope("barrier"):
+        pl.semaphore_wait(barrier, groups + has_next.astype(jnp.int32) + has_previous.astype(jnp.int32))
+
+    gain_copy.wait()
+    gain_pieces[parity] = gain_raw[...].astype(jnp.float32)
+    gain_send.start()
+    ids_copy.wait()
+    ids_send.start()
     for j in range(tiles):
         tile_copy(j).start()
-    cosine_copy.start()
-    sine_copy.start()
     for c in range(chunks):
         chunk_copy(c).start()
 
@@ -154,27 +179,6 @@
         fresh_ids_copy.start()
         for c in range(chunks):
             fresh_copy(c).start()
-
-    barrier = pltpu.get_barrier_semaphore()
-    pl.semaphore_signal(barrier, inc=1, device_id=core, device_id_type=MESH)
-    for g in range(1, groups):
-        pl.semaphore_signal(barrier, inc=1, device_id=(place, peer(g)), device_id_type=MESH)
-
-    @pl.when(has_next)
-    def _():
-        pl.semaphore_signal(barrier, inc=1, device_id=ahead, device_id_type=MESH)
-
-    @pl.when(has_previous)
-    def _():
-        pl.semaphore_signal(barrier, inc=1, device_id=behind, device_id_type=MESH)
-
-    pl.semaphore_wait(barrier, groups + has_next.astype(jnp.int32) + has_previous.astype(jnp.int32))
-
-    gain_copy.wait()
-    gain_pieces[parity] = gain_raw[...].astype(jnp.float32)
-    gain_send.start()
-    ids_copy.wait()
-    ids_send.start()
 
     def normalize(step):
         def some(r, carry):
@@ -217,10 +221,10 @@
             share_copy(g, s).wait_recv()
             relay_copy(g, s, h).start()
 
-    def project(rows, places, first, events):
+    def project(rows, places, first=False, events=(), gate=True):
         def one(j, carry):
             for at, event in events:
-                pl.when(j == at)(event)
+                pl.when((j == min(at, tiles - 1)) & gate)(event)
             if first:
                 tile_copy(j).wait()
             kind = j // per_kind
@@ -241,14 +245,14 @@
 
         lax.fori_loop(0, tiles, one, 0)
 
-    def project_others(h):
+    def project_others(h, events=()):
         def one(g, carry):
             index = source(g)
             project(
                 lambda: gathered[index, h * block : (h + 1) * block, :],
                 [h * half + index * block],
-                False,
-                [],
+                events=events,
+                gate=g == 1,
             )
             return carry
 
@@ -270,7 +274,7 @@
                         seen = seen & (lax.broadcasted_iota(jnp.int32, (LANES, LANES), 1) <= down)
                     bias[first : first + LANES, k * LANES : (k + 1) * LANES] = jnp.where(seen, 0.0, -1e30)
 
-    def attend(h):
+    def attend(h, low, high):
         def one(n, carry):
             to = pl.ds(pl.multiple_of(n * HD, HD), HD)
             for q in range(half // LANES):
@@ -290,61 +294,52 @@
                 mixed[q * LANES : (q + 1) * LANES, to] = (product / total).astype(jnp.bfloat16)
             return carry
 
-        lax.fori_loop(0, heads, one, 0, unroll=2)
-
-    def give_copy(i):
-        g, c = (i // chunks + 1) % groups, i % chunks
-        slot = i % 2
+        lax.fori_loop(low, high, one, 0, unroll=min(4, high - low))
+
+    def give_copy(c):
+        return remote(partial.at[c], give_in.at[c], give_send.at[c], give_recv.at[c], core)
+
+    def out_products(c):
+        for n in range(0, chunk, PIECE):
+            columns = slice(n, n + PIECE)
+            yield columns, jnp.dot(mixed[...], weights_out[c, :, columns], preferred_element_type=jnp.float32)
+
+    def give(low, high):
+        def one(c, carry):
+            for columns, product in out_products(c):
+                partial[c, :, columns] = product.astype(jnp.bfloat16)
+            give_copy(c).start()
+            return carry
+
+        lax.fori_loop(low, high, one, 0)
+
+    def wait_given():
+        wait_sent([give_copy(c) for c in range(chunks)])
+
+    def multiply():
+        def one(c, carry):
+            for columns, product in out_products(c):
+                partial[c, :, columns] = product.astype(jnp.bfloat16)
+            return carry
+
+        lax.fori_loop(0, chunks, one, 0)
+
+    def sum_copy(g, c):
+        slot = (g - 1) * chunks + c
         return remote(
-            give_out.at[slot], give_in.at[c, block_at(peer(g))], give_send.at[slot], give_recv.at[i], core
+            give_in.at[c, block_at(peer(g))], arrived.at[c, g - 1], sum_send.at[slot], sum_recv.at[slot], (place, peer(g))
         )
 
-    def out_product(i):
-        g, c = (i // chunks + 1) % groups, i % chunks
-        return jnp.dot(mixed[block_at(peer(g)), :], weights_out[c], preferred_element_type=jnp.float32)
-
-    messages = groups * chunks
-
-    def give():
-        def one(i, carry):
-            @pl.when(i >= 2)
-            def _():
-                give_copy(i).wait_send()
-
-            give_out[i % 2] = out_product(i).astype(jnp.bfloat16)
-            give_copy(i).start()
+    def combine(low, high):
+        def one(c, carry):
+            give_copy(c).wait_recv()
+            total = partial[c].astype(jnp.float32) + give_in[c].astype(jnp.float32)
+            give_in[c] = total.astype(jnp.bfloat16)
+            for g in range(1, groups):
+                sum_copy(g, c).start()
             return carry
 
-        lax.fori_loop(0, messages, one, 0)
-        give_copy(messages - 2).wait_send()
-        give_copy(messages - 1).wait_send()
-
-    def sum_copy(i):
-        g, c = i // chunks + 1, i % chunks
-        return remote(
-            give_in.at[c, block_at(peer(g))], arrived.at[c, g - 1], sum_send.at[i], sum_recv.at[i], (place, peer(g))
-        )
-
-    def keep_others():
-        def one(i, carry):
-            g, c = i // chunks + 1, i % chunks
-            give_copy(i).wait_recv()
-            total = out_product(i) + give_in[c, block_at(peer(g)), :].astype(jnp.float32)
-            give_in[c, block_at(peer(g)), :] = total.astype(jnp.bfloat16)
-            sum_copy(i).start()
-            return carry
-
-        lax.fori_loop(0, messages - chunks, one, 0)
-
-    def keep_own(step):
-        def one(i, carry):
-            c = i % chunks
-            give_copy(i).wait_recv()
-            total = out_product(i) + give_in[c, block_at(mine), :].astype(jnp.float32)
-            kept[c] = total + rows_in[step, c].astype(jnp.float32)
-            return carry
-
-        lax.fori_loop(messages - chunks, messages, one, 0)
+        lax.fori_loop(low, high, one, 0)
 
     def store_copy(step, c):
         return pltpu.make_async_copy(staged.at[c], out_hbm.at[step, 0, :, columns_of(c)], store_sem.at[c])
@@ -359,10 +354,13 @@
 
     def finish(step, low, high):
         def one(c, carry):
-            total = kept[c]
+            total = rows_in[step, c].astype(jnp.float32) + give_in[c, block_at(mine), :].astype(jnp.float32)
             for g in range(1, groups):
-                sum_copy((g - 1) * chunks + c).wait_recv()
+                sum_copy(g, c).wait_recv()
                 total = total + arrived[c, g - 1].astype(jnp.float32)
+            if step > 0:
+                store_copy(0, c).wait()
+                pl.when(has_next)(lambda: shift_copy(c).wait_send())
             staged[c] = total.astype(jnp.bfloat16)
             if step == 0:
                 pl.when(has_next)(lambda: shift_copy(c).start())
@@ -383,6 +381,7 @@
     every_share = [(g, s) for g in range(1, groups) for s in range(PARTS)]
     is_low, is_high = parity == 0, parity == 1
 
+    scope = jax.named_scope
     ids_send.wait_recv()
     ids[0, 0:1, :] = pieces[0]
     ids[0, 1:2, :] = pieces[1]
@@ -392,7 +391,8 @@
     gain[:, depth // 2 :] = gain_pieces[1]
     for c in range(chunks):
         own_rows_copy(c).wait()
-    normalize(0)
+    with scope("norm"):
+        normalize(0)
     own_copy().start()
     pl.when(is_low)(share)
 
@@ -404,25 +404,63 @@
 
     cosine_copy.wait()
     sine_copy.wait()
-    find_bias(0)
+    with scope("bias"):
+        find_bias(0)
+
+    def relay_low(s):
+        with scope("early_relay"):
+            pl.when(is_low)(lambda: relay(s, 0))
+
+    def combine_low(c):
+        with scope("combine"):
+            pl.when(is_low)(lambda: combine(c, c + 1))
+
+    def finish_low(step, c):
+        with scope("finish"):
+            pl.when(is_low)(lambda: finish(step, c, c + 1))
+
+    def free_link():
+        @pl.when(is_high)
+        def _():
+            with scope("finish"):
+                finish(0, chunks - 2, chunks - 1)
+                wait_sent([sum_copy(g, c) for g in range(1, groups) for c in range(chunks - 1)])
+            pl.semaphore_signal(free_sem, inc=1, device_id=core, device_id_type=MESH)
+
+    def share_low():
+        @pl.when(is_low)
+        def _():
+            with scope("wait_free"):
+                pl.semaphore_wait(free_sem, 1)
+            share()
+
+    def next_rows():
+        @pl.when(has_previous)
+        def _():
+            with scope("wait_shift"):
+                ids_ahead.wait_recv()
+                for c in range(chunks):
+                    shift_copy(c).wait_recv()
+
+        @pl.when(jnp.logical_not(has_previous))
+        def _():
+            fresh_ids_copy.wait()
+            for c in range(chunks):
+                fresh_copy(c).wait()
+
+        own_copy().wait_send()
+        wait_sent([share_copy(g, s) for g, s in every_share])
+        with scope("norm"):
+            normalize(1)
+        own_copy().start()
 
     for step in range(2):
-        own_copy().wait_recv()
-
-        def send_high():
-            pl.when(is_high)(share)
-
-        def relay_low():
-            pl.when(is_low)(lambda: relay(0, 0))
-
-        project(
-            lambda: gathered[mine],
-            [mine * block, half + mine * block],
-            step == 0,
-            [(min(RELAY_AT, tiles - 1), relay_low), (min(SEND_AT, tiles - 1), send_high)],
-        )
-
+        relays = [(at, functools.partial(relay_low, s)) for s, at in enumerate(RELAYS_AT[step])]
         if step == 0:
+            with scope("wait_own"):
+                own_copy().wait_recv()
+            with scope("own"):
+                project(lambda: gathered[mine], [mine * block, half + mine * block], True, relays)
 
             @pl.when(jnp.logical_not(has_next))
             def _():
@@ -431,99 +469,136 @@
 
             for c in range(chunks):
                 chunk_copy(c).wait()
-
-        @pl.when(is_low)
-        def _():
-            for s in range(1, PARTS):
-                relay(s, 0)
-
-        @pl.when(is_high)
-        def _():
-            for g, s in every_share:
-                relay_copy(g, s, 0).wait_recv()
-
-        project_others(0)
-        attend(0)
-
-        @pl.when(is_low)
-        def _():
-            wait_sent([relay_copy(g, s, 0) for g, s in every_share])
-            keep_others()
-            keep_own(step)
-
-        @pl.when(is_high)
-        def _():
-            give()
-            for s in range(PARTS):
-                relay(s, 1)
-
-        @pl.when(is_low)
-        def _():
-            for g, s in every_share:
-                relay_copy(g, s, 1).wait_recv()
-
-        project_others(1)
-
-        @pl.when(is_low)
-        def _():
-            finish(step, 0, 2)
-
-        attend(1)
-
-        @pl.when(is_low)
-        def _():
-            give()
-            finish(step, 2, chunks)
-
-        @pl.when(is_high)
-        def _():
-            wait_sent([relay_copy(g, s, 1) for g, s in every_share])
-            keep_others()
-            keep_own(step)
-            finish(step, 0, chunks)
-
-        wait_sent([sum_copy(i) for i in range(messages - chunks)])
-        if step == 0:
+        else:
+
+            @pl.when(is_low)
+            def _():
+                wait_sent([sum_copy(g, c) for g in range(1, groups) for c in range(chunks)])
+                next_rows()
 
             @pl.when(is_high)
             def _():
-                pl.semaphore_signal(free_sem, inc=1, device_id=core, device_id_type=MESH)
-
-        own_copy().wait_send()
-        wait_sent([share_copy(g, s) for g, s in every_share])
-        for c in range(chunks):
-            store_copy(step, c).wait()
-        if step == 0:
-
-            @pl.when(has_next)
-            def _():
-                ids_ahead.wait_send()
-                wait_sent([shift_copy(c) for c in range(chunks)])
-
-            @pl.when(has_previous)
-            def _():
-                ids_ahead.wait_recv()
-                for c in range(chunks):
-                    shift_copy(c).wait_recv()
-
-            @pl.when(jnp.logical_not(has_previous))
-            def _():
-                fresh_ids_copy.wait()
-                for c in range(chunks):
-                    fresh_copy(c).wait()
-
-            normalize(1)
-            own_copy().start()
+                with scope("finish"):
+                    finish(0, 0, chunks - 2)
+                with scope("wait_own"):
+                    own_copy().wait_recv()
+
+            with scope("own_low"):
+                project(
+                    lambda: gathered[mine, 0:block, :],
+                    [mine * block],
+                    events=[(FREE_AT, free_link), (SHARE_AT, share_low)],
+                )
 
             @pl.when(is_low)
             def _():
-                pl.semaphore_wait(free_sem, 1)
-                share()
-
-            find_bias(1)
-
+                find_bias(1)
+                with scope("wait_own"):
+                    own_copy().wait_recv()
+
+            @pl.when(is_high)
+            def _():
+                with scope("finish"):
+                    finish(0, chunks - 1, chunks)
+                wait_sent([sum_copy(g, chunks - 1) for g in range(1, groups)])
+                next_rows()
+                find_bias(1)
+
+            with scope("own_high"):
+                project(lambda: gathered[mine, block:, :], [half + mine * block], events=relays)
+
+        @pl.when(is_low)
+        def _():
+            with scope("late_relay"):
+                for s in range(len(RELAYS_AT[step]), PARTS):
+                    relay(s, 0)
+
+        @pl.when(is_high)
+        def _():
+            with scope("wait_relay"):
+                for s in range(PARTS):
+                    for g in range(1, groups):
+                        relay_copy(g, s, 0).wait_recv()
+                    if s == PARTS - 2:
+                        share()
+
+        with scope("others"):
+            project_others(0)
+        with scope("attend"):
+            attend(0, 0, heads)
+
+        @pl.when(is_low)
+        def _():
+            wait_sent([relay_copy(g, s, 0) for g, s in every_share])
+            if step > 0:
+                wait_given()
+            with scope("multiply"):
+                multiply()
+            with scope("combine"):
+                combine(0, chunks - len(COMBINES_AT))
+            with scope("wait_relay"):
+                for g, s in every_share:
+                    relay_copy(g, s, 1).wait_recv()
+
+        @pl.when(is_high)
+        def _():
+            with scope("relay_high"):
+                for s in range(PARTS - 1):
+                    relay(s, 1)
+            with scope("give"):
+                give(0, 3)
+            with scope("relay_high"):
+                relay(PARTS - 1, 1)
+            with scope("give"):
+                give(3, chunks)
+
+        with scope("others"):
+            late = chunks - len(COMBINES_AT)
+            events = [(at, functools.partial(combine_low, late + i)) for i, at in enumerate(COMBINES_AT)]
+            project_others(1, [*events, (FINISH_AT, functools.partial(finish_low, step, 0))])
+        finish_low(step, 1)
+        with scope("attend"):
+            attend(1, 0, heads // 2)
+        finish_low(step, 2)
+        with scope("attend"):
+            attend(1, heads // 2, heads)
+
+        @pl.when(is_low)
+        def _():
+            with scope("give"):
+                give(0, 2)
+        finish_low(step, 3)
+
+        @pl.when(is_low)
+        def _():
+            with scope("give"):
+                give(2, chunks)
+            with scope("finish"):
+                finish(step, 4, chunks)
+
+        @pl.when(is_high)
+        def _():
+            wait_sent([relay_copy(g, s, 1) for g, s in every_share])
+            wait_given()
+            with scope("multiply"):
+                multiply()
+            with scope("combine"):
+                combine(0, chunks)
+
+    @pl.when(is_high)
+    def _():
+        with scope("finish"):
+            finish(1, 0, chunks)
+
+    pl.when(is_low)(wait_given)
+    wait_sent([sum_copy(g, c) for g in range(1, groups) for c in range(chunks)])
+    own_copy().wait_send()
+    wait_sent([share_copy(g, s) for g, s in every_share])
     gain_send.wait_send()
     ids_send.wait_send()
+    pl.when(has_next)(ids_ahead.wait_send)
+    for c in range(chunks):
+        store_copy(1, c).wait()
 
     @pl.when(has_previous)
     def _():
@@ -531,8 +606,9 @@
 
     @pl.when(has_next)
     def _():
-        for c in range(chunks):
-            back_copy(c).wait_recv()
+        with scope("wait_back"):
+            for c in range(chunks):
+                back_copy(c).wait_recv()
 
 
 def turning(tokens):
@@ -560,7 +636,7 @@
     near, f32 = jnp.bfloat16, jnp.float32
     dma = pltpu.SemaphoreType.DMA
     shares = (groups - 1) * PARTS
-    messages = groups * chunks
+    sums = (groups - 1) * chunks
     flops = 2 * (2 * 2 * half * depth * 4 * width + 4 * width * 4 * half * half)
     out, shadow = pl.pallas_call(
         functools.partial(relay_kernel, groups, sections),
@@ -576,8 +652,7 @@
             pltpu.VMEM((groups, 2 * block, depth), near),
             pltpu.VMEM((3, 2 * half, width), near),
             pltpu.VMEM((half, width), near),
-            pltpu.VMEM((chunks, block, CHUNK), f32),
-            pltpu.VMEM((2, block, CHUNK), near),
+            pltpu.VMEM((chunks, half, CHUNK), near),
             pltpu.VMEM((chunks, half, CHUNK), near),
             pltpu.VMEM((chunks, groups - 1, block, CHUNK), near),
             pltpu.VMEM((2, chunks, block, CHUNK), near),
@@ -603,10 +678,10 @@
             dma((shares,)),
             dma((shares,)),
             dma((shares,)),
-            dma((2,)),
-            dma((messages,)),
-            dma((messages - chunks,)),
-            dma((messages - chunks,)),
+            dma((chunks,)),
+            dma((chunks,)),
+            dma((sums,)),
+            dma((sums,)),
             dma((chunks,)),
             dma((chunks,)),
             dma((chunks,)),

time: 180 us -> 140 us (0.78)
  Pallas kernels: 175 us -> 134 us
    pallas_call x1, Pallas kernels: 175 us -> 134 us  [per_device(): pl.pallas_call(functools.partial(relay_kernel, groups, sections), out_sha...]
where the time goes in v1:
time: 140 us; the launch traced here: 139 us
  Pallas kernels  134 us (96%)
  local copies, waits for them, and re-layouts  4.56 us (3%)
    pallas_call x1, Pallas kernels, per_device(): pl.pallas_call(functools.partial(relay_kernel, groups, sections), out_sha...  134 us
    unnamed x4, local copies, waits for them, and re-layouts  4.56 us

profile of v1, /device:TPU:1, one launch (start us, length us, event | category | flops | bytes accessed | tf_op | source)
XLA Modules:
  0.0 139.1 jit_solution(9244315476663820933)
XLA Ops:
  0.6 133.9 %relay.1 = (bf16[2,1,128,5120]{3,2,1,0:T(8,128)(2,1)}, bf16[1,128,5120]{2,1,0:T(8,128)(2,1)}) custom-call(bf16[128,5120]{1,0:T(8,128)(2,1)} %bitcast.7, s32[1,256]{1,0:T(1,128)} %segments_hbm.1, bf16[2,128,5120]{2,1,0:T(8,128)(2,1)} %fresh_hbm.1, s32[2,256]{1,0:T(2,128)} %fresh_segments_hbm.1, bf16[3,5120,1024]{2,1,0:T(8,128)(2,1)} %bitcast.5, ...), custom_call_target="tpu_custom_call" | custom-call | flops 45097156608 | bytes 41943040 | tf_op jit(solution)/shard_map/relay/pallas_call | solution.py:641
  134.5 0.0 copy-start
  134.5 3.5 %copy.13 = bf16[2,1,128,5120]{3,2,1,0:T(8,128)(2,1)} copy(bf16[2,1,128,5120]{3,2,1,0:T(8,128)(2,1)} %get-tuple-element.4) | data formatting | bytes 5242880
  138.0 0.0 copy-done
  138.0 1.1 copy.14
Async XLA Ops:
  134.5 3.5 %copy-start = (bf16[1,128,5120]{2,1,0:T(8,128)(2,1)S(1)}, bf16[1,128,5120]{2,1,0:T(8,128)(2,1)}, u32[]{:S(2)}) copy-start(bf16[1,128,5120]{2,1,0:T(8,128)(2,1)} %get-tuple-element.5) | copy-start | bytes 3932164

commit v2 on v1

--- a/solution.py
+++ b/solution.py
@@ -13,12 +13,15 @@
 LOG2E = 1.4426950408889634
 TILE = 512
 CHUNK = 1024
+UNIT = 1
 PARTS = 4
 NORM_ROWS = 16
 PIECE = 256
-RELAYS_AT = ((3, 5), (0, 0, 3))
+PIECES = 4
+RELAYS_AT = ((3, 5), (0, 0, 3, 5))
 COMBINES_AT = (1, 2, 3)
 FREE_AT = 3
+LAST_AT = 5
 SHARE_AT = 4
 FINISH_AT = 4
 MESH = pl.DeviceIdType.MESH
@@ -39,7 +42,8 @@
     gain_hbm,
     cosine_hbm,
     sine_hbm,
-    out_hbm,
+    first_hbm,
+    second_hbm,
     shadow_hbm,
     weights_in,
     weights_out,
@@ -342,7 +346,8 @@
         lax.fori_loop(low, high, one, 0)
 
     def store_copy(step, c):
-        return pltpu.make_async_copy(staged.at[c], out_hbm.at[step, 0, :, columns_of(c)], store_sem.at[c])
+        out = second_hbm if step else first_hbm
+        return pltpu.make_async_copy(staged.at[c], out.at[:, columns_of(c)], store_sem.at[c])
 
     def shift_copy(c):
         return remote(staged.at[c], rows_in.at[1, c], shift_send.at[c], shift_recv.at[c], ahead)
@@ -411,13 +416,17 @@
         with scope("early_relay"):
             pl.when(is_low)(lambda: relay(s, 0))
 
-    def combine_low(c):
+    def combine_low(u):
         with scope("combine"):
-            pl.when(is_low)(lambda: combine(c, c + 1))
-
-    def finish_low(step, c):
+            pl.when(is_low)(lambda: combine(u * UNIT, (u + 1) * UNIT))
+
+    def finish_low(step, u):
         with scope("finish"):
-            pl.when(is_low)(lambda: finish(step, c, c + 1))
+            pl.when(is_low)(lambda: finish(step, u * UNIT, (u + 1) * UNIT))
+
+    def finish_last():
+        with scope("finish"):
+            pl.when(is_high)(lambda: finish(0, chunks - 1, chunks))
 
     def free_link():
         @pl.when(is_high)
@@ -487,7 +496,7 @@
                 project(
                     lambda: gathered[mine, 0:block, :],
                     [mine * block],
-                    events=[(FREE_AT, free_link), (SHARE_AT, share_low)],
+                    events=[(FREE_AT, free_link), (LAST_AT, finish_last), (SHARE_AT, share_low)],
                 )
 
             @pl.when(is_low)
@@ -498,8 +507,6 @@
 
             @pl.when(is_high)
             def _():
-                with scope("finish"):
-                    finish(0, chunks - 1, chunks)
                 wait_sent([sum_copy(g, chunks - 1) for g in range(1, groups)])
                 next_rows()
                 find_bias(1)
@@ -535,7 +542,7 @@
             with scope("multiply"):
                 multiply()
             with scope("combine"):
-                combine(0, chunks - len(COMBINES_AT))
+                combine(0, chunks - UNIT * len(COMBINES_AT))
             with scope("wait_relay"):
                 for g, s in every_share:
                     relay_copy(g, s, 1).wait_recv()
@@ -546,14 +553,14 @@
                 for s in range(PARTS - 1):
                     relay(s, 1)
             with scope("give"):
-                give(0, 3)
+                give(0, 3 * UNIT)
             with scope("relay_high"):
                 relay(PARTS - 1, 1)
             with scope("give"):
-                give(3, chunks)
+                give(3 * UNIT, chunks)
 
         with scope("others"):
-            late = chunks - len(COMBINES_AT)
+            late = chunks // UNIT - len(COMBINES_AT)
             events = [(at, functools.partial(combine_low, late + i)) for i, at in enumerate(COMBINES_AT)]
             project_others(1, [*events, (FINISH_AT, functools.partial(finish_low, step, 0))])
         finish_low(step, 1)
@@ -566,15 +573,15 @@
         @pl.when(is_low)
         def _():
             with scope("give"):
-                give(0, 2)
+                give(0, 2 * UNIT)
         finish_low(step, 3)
 
         @pl.when(is_low)
         def _():
             with scope("give"):
-                give(2, chunks)
+                give(2 * UNIT, chunks)
             with scope("finish"):
-                finish(step, 4, chunks)
+                finish(step, 4 * UNIT, chunks)
 
         @pl.when(is_high)
         def _():
@@ -609,6 +616,44 @@
         with scope("wait_back"):
             for c in range(chunks):
                 back_copy(c).wait_recv()
+
+
+def collect_kernel(first, second, shadow, out, back, held, load_sem, store_sem):
+    rows = first.shape[0] // PIECES
+    moves = []
+    for source, target in ((first, out.at[0, 0]), (second, out.at[1, 0]), (shadow.at[0], back.at[0])):
+        for n in range(PIECES):
+            part, slot = pl.ds(n * rows, rows), len(moves)
+            load = pltpu.make_async_copy(source.at[part], held.at[slot], load_sem.at[slot])
+            store = pltpu.make_async_copy(held.at[slot], target.at[part], store_sem.at[slot])
+            load.start()
+            moves.append((load, store))
+    for load, store in moves:
+        load.wait()
+        store.start()
+    for _, store in moves:
+        store.wait()
+
+
+def collect(first, second, shadow):
+    block, depth = first.shape
+    near, count = first.dtype, 3 * PIECES
+    return pl.pallas_call(
+        collect_kernel,
+        out_shape=(
+            jax.ShapeDtypeStruct((2, 1, block, depth), near),
+            jax.ShapeDtypeStruct((1, block, depth), near),
+        ),
+        in_specs=[pl.BlockSpec(memory_space=pl.ANY)] * 3,
+        out_specs=(pl.BlockSpec(memory_space=pl.ANY),) * 2,
+        scratch_shapes=[
+            pltpu.VMEM((count, block // PIECES, depth), near),
+            pltpu.SemaphoreType.DMA((count,)),
+            pltpu.SemaphoreType.DMA((count,)),
+        ],
+        compiler_params=pltpu.CompilerParams(vmem_limit_bytes=67043328),
+        name="collect",
+    )(first, second, shadow)
 
 
 def turning(tokens):
@@ -638,14 +683,15 @@
     shares = (groups - 1) * PARTS
     sums = (groups - 1) * chunks
     flops = 2 * (2 * 2 * half * depth * 4 * width + 4 * width * 4 * half * half)
-    out, shadow = pl.pallas_call(
+    first, second, shadow = pl.pallas_call(
         functools.partial(relay_kernel, groups, sections),
         out_shape=(
-            jax.ShapeDtypeStruct((2, 1, block, depth), near),
+            jax.ShapeDtypeStruct((block, depth), near),
+            jax.ShapeDtypeStruct((block, depth), near),
             jax.ShapeDtypeStruct((1, block, depth), near),
         ),
         in_specs=[pl.BlockSpec(memory_space=pl.ANY)] * 9,
-        out_specs=(pl.BlockSpec(memory_space=pl.ANY),) * 2,
+        out_specs=(pl.BlockSpec(memory_space=pl.ANY),) * 3,
         scratch_shapes=[
             pltpu.VMEM((tiles, depth, tile), near),
             pltpu.VMEM((chunks, width, CHUNK), near),
@@ -707,7 +753,7 @@
         cosine,
         sine,
     )
-    return out, shadow
+    return collect(first, second, shadow)
 
 
 def solution(mesh):

time: 140 us -> 138 us (0.986)
  local copies, waits for them, and re-layouts: 4.56 us -> 0 us
  Pallas kernels: 134 us -> 137 us
    unnamed x4 -> x0, local copies, waits for them, and re-layouts: 4.56 us -> none
    pallas_call x0 -> x1, Pallas kernels: none -> 3.47 us  [collect(): pl.pallas_call(collect_kernel, out_shape=(jax.ShapeDtypeStruct((2, 1, blo...]
where the time goes in v2:
time: 138 us
  Pallas kernels  137 us (99%)
    pallas_call x1, Pallas kernels, per_device(): pl.pallas_call(functools.partial(relay_kernel, groups, sections), out_sha...  134 us
    pallas_call x1, Pallas kernels, collect(): pl.pallas_call(collect_kernel, out_shape=(jax.ShapeDtypeStruct((2, 1, blo...  3.47 us

profile of v2, /device:TPU:1, one launch (start us, length us, event | category | flops | bytes accessed | tf_op | source)
XLA Modules:
  0.0 138.3 jit_solution(13630756768870470321)
XLA Ops:
  0.6 134.0 %relay.1 = (bf16[128,5120]{1,0:T(8,128)(2,1)}, bf16[128,5120]{1,0:T(8,128)(2,1)}, bf16[1,128,5120]{2,1,0:T(8,128)(2,1)}) custom-call(bf16[128,5120]{1,0:T(8,128)(2,1)} %bitcast.7, s32[1,256]{1,0:T(1,128)} %segments_hbm.1, bf16[2,128,5120]{2,1,0:T(8,128)(2,1)} %fresh_hbm.1, s32[2,256]{1,0:T(2,128)} %fresh_segments_hbm.1, bf16[3,5120,1024]{2,1,0:T(8,128)(2,1)} %bitcast.5, ...), custom_call_target="tpu_custom_call" | custom-call | flops 45097156608 | bytes 41943040 | tf_op jit(solution)/shard_map/relay/pallas_call | solution.py:686
  134.6 3.5 %collect.1 = (bf16[2,1,128,5120]{3,2,1,0:T(8,128)(2,1)}, bf16[1,128,5120]{2,1,0:T(8,128)(2,1)}) custom-call(bf16[128,5120]{1,0:T(8,128)(2,1)} %get-tuple-element.5.first, bf16[128,5120]{1,0:T(8,128)(2,1)} %get-tuple-element.6.second, bf16[1,128,5120]{2,1,0:T(8,128)(2,1)} %get-tuple-element.7.shadow), custom_call_target="tpu_custom_call" | custom-call | tf_op jit(solution)/shard_map/collect/pallas_call | solution.py:641
